TPU v7x, 128 devices: a whole 4x4x4 slice. The times are simulated.
128 devices in a mesh: row: 8 (over y, core), col: 16 (over z, x).
Axes of the slice: x: 4, y: 4, z: 4, core: 2. Of those that a mesh axis runs over, the one named last changes fastest.
Arguments:
- images: bfloat16 [16384, 768], P(('row', 'col')), may hold values from -5 to 5
- texts: bfloat16 [16384, 768], P(('col', 'row')), may hold values from -5 to 5
- audio: bfloat16 [16384, 768], P(('col', 'row')), may hold values from -5 to 5
Outputs:
- grad_images: float32 [16384, 768], P(('row', 'col'))
- grad_texts: float32 [16384, 768], P(('col', 'row'))
- grad_audio: float32 [16384, 768], P(('col', 'row'))
All inputs are finite; a program needn't handle non-finite values.
Results may differ from a plain program's by a relative error of at most 0.013.
Values may be sent and summed in bfloat16 or wider, within the bound.
A program may use at most 128 MiB of HBM per device.

v0:
```python
import jax
import jax.numpy as jnp
from jax import lax
from jax.sharding import Mesh
from jax.sharding import PartitionSpec as P

ITERS = 3
COL = ("col_0", "col_1")
ROW_COL = ("row", "col_0", "col_1")
COL_ROW = ("col_0", "col_1", "row")
logit_softness = 0.07
target_softness = 0.05
epsilon = 1e-06


def in_one_piece(arrays, axis, dim, along):
    both = jnp.concatenate(arrays, axis=along)
    filled, at, outs = (lax.all_gather(both, axis, axis=dim, tiled=True), 0, [])
    for a in arrays:
        outs.append(lax.slice_in_dim(filled, at, at + a.shape[along], axis=along))
        at += a.shape[along]
    return tuple(outs)


def from_everyone(value, axis):
    size = lax.axis_size(axis)
    return lax.all_to_all(
        jnp.broadcast_to(value[None], (size, *value.shape)), axis, 0, 0, tiled=True
    )


def taken_together(value, axis):
    everything = from_everyone(value, axis)
    return jnp.sum(everything, axis=0)


def in_one(arrays, axis):
    ends = [0]
    for a in arrays:
        ends.append(ends[-1] + a.size)
    subtotal = taken_together(jnp.concatenate([a.ravel() for a in arrays]), axis)
    return tuple((subtotal[b:e].reshape(a.shape) for a, b, e in zip(arrays, ends, ends[1:])))


def summed_rows(terms, axes):
    subtotal = terms.astype(jnp.bfloat16)
    for axis in axes:
        subtotal = lax.psum_scatter(subtotal, axis, scatter_dimension=0, tiled=True)
    return subtotal.astype(jnp.float32)


def cut_along(value, dim, size):
    shape = value.shape
    blocks = value.reshape(*shape[:dim], size, shape[dim] // size, *shape[dim + 1 :])
    return jnp.moveaxis(blocks, dim, 0)


def summed_on_arrival(value, axis, dim):
    blocks = cut_along(value, dim, lax.axis_size(axis))
    arrived = lax.all_to_all(blocks, axis, split_axis=0, concat_axis=0, tiled=True)
    return arrived.astype(jnp.float32).sum(axis=0)


def normalize(raw):
    values = raw.astype(jnp.float32)
    inverse = lax.rsqrt(jnp.sum(values * values, axis=1, keepdims=True) + epsilon)
    return (values * inverse, inverse)


def backward(unit, inverse, incoming):
    return (incoming - unit * jnp.sum(unit * incoming, axis=1, keepdims=True)) * inverse


def shards(images, texts, audio):
    img_unit, img_inverse = normalize(images)
    txt_unit, txt_inverse = normalize(texts)
    aud_unit, aud_inverse = normalize(audio)
    img_rows = lax.all_gather(img_unit.astype(jnp.bfloat16), COL, axis=0, tiled=True)
    text_columns, audio_columns = in_one_piece(
        (txt_unit.astype(jnp.bfloat16), aud_unit.astype(jnp.bfloat16)), "row", 0, 1
    )
    paired_cols = jnp.concatenate([text_columns, audio_columns], axis=0)
    contract = (((1,), (1,)), ((), ()))
    cosine_matrix = lax.dot_general(
        img_rows, paired_cols, contract, preferred_element_type=jnp.float32
    )
    row_extent = img_rows.shape[0]
    column_width = text_columns.shape[0]
    loss_routine = jnp.exp(cosine_matrix / target_softness).reshape(row_extent, 2, column_width)
    softmax_exponent = jnp.exp(cosine_matrix / logit_softness).reshape(row_extent, 2, column_width)
    cols_scale = jnp.ones((2, column_width), jnp.float32)
    opening = 0
    row_sums, row_total = in_one(
        (jnp.sum(loss_routine * cols_scale[None], axis=2), jnp.sum(softmax_exponent, axis=2)), COL
    )
    rows_scale = 1.0 / row_sums
    col_sums, col_total = in_one(
        (jnp.sum(loss_routine * rows_scale[:, :, None], axis=0), jnp.sum(softmax_exponent, axis=0)),
        "row",
    )
    cols_scale = 1.0 / col_sums
    opening = 1
    for iteration in range(opening, ITERS):
        row_sums = taken_together(jnp.sum(loss_routine * cols_scale[None], axis=2), COL)
        rows_scale = 1.0 / row_sums
        col_sums = taken_together(jnp.sum(loss_routine * rows_scale[:, :, None], axis=0), "row")
        cols_scale = 1.0 / col_sums
    target = loss_routine * rows_scale[:, :, None] * cols_scale[None]
    row_mass = taken_together(jnp.sum(target, axis=2), COL)
    score_grad = (
        softmax_exponent / row_total[:, :, None] * row_mass[:, :, None]
        - target
        + softmax_exponent / col_total[None]
        - target
    )
    score_matrix = score_grad.astype(jnp.bfloat16).reshape(row_extent, 2 * column_width)
    owned = images.shape[0]
    image_gradient = summed_rows(
        jnp.dot(score_matrix, paired_cols, preferred_element_type=jnp.float32) / logit_softness, COL
    )
    text_part = lax.slice_in_dim(score_matrix, 0, owned * lax.axis_size("row"), axis=1)
    audio_part = lax.dynamic_slice_in_dim(
        score_matrix, column_width, owned * lax.axis_size("row"), 1
    )
    down = (((0,), (0,)), ((), ()))
    text_gradient_out = lax.dot_general(
        text_part, img_rows, down, preferred_element_type=jnp.float32
    )
    audio_gradient_out = lax.dot_general(
        audio_part, img_rows, down, preferred_element_type=jnp.float32
    )
    paired_grad = summed_on_arrival(
        (jnp.concatenate([text_gradient_out, audio_gradient_out], axis=1) / logit_softness).astype(
            jnp.bfloat16
        ),
        "row",
        0,
    )
    width = images.shape[1]
    grad_txt = backward(txt_unit, txt_inverse, paired_grad[:, :width])
    grad_aud = backward(aud_unit, aud_inverse, paired_grad[:, width:])
    return (backward(img_unit, img_inverse, image_gradient), grad_txt, grad_aud)


def solution(mesh):
    split = Mesh(mesh.devices.reshape(mesh.shape["row"], 4, 4), ("row", "col_0", "col_1"))
    placed = (P(ROW_COL, None), P(COL_ROW, None), P(COL_ROW, None))
    return jax.shard_map(
        shards,
        mesh=split,
        in_specs=placed,
        out_specs=(P(ROW_COL, None), P(COL_ROW, None), P(COL_ROW, None)),
        check_vma=False,
    )
```

profile of v0, /device:TPU:0, one launch (start us, length us, event | category | flops | bytes accessed | tf_op | source)
XLA Modules:
  0.0 329.2 jit_solution(17503242842045232137)
XLA Ops:
  14.1 27.5 %all-gather.5.cloned.1.call-done = bf16[1024,1536]{1,0:T(8,128)(2,1)} async-done(((bf16[128,1536]{1,0:T(8,128)(2,1)}), bf16[1024,1536]{1,0:T(8,128)(2,1)}) %all-gather.5.cloned.1.call-update) | async-done | bytes 3145744 | tf_op jit(solution)/shard_map/all_gather | solution.py:18
  44.9 47.4 %all-gather.3.cloned.1.call-done = bf16[2048,768]{1,0:T(8,128)(2,1)} async-done(((bf16[128,768]{1,0:T(8,128)(2,1)}), bf16[2048,768]{1,0:T(8,128)(2,1)}) %all-gather.3.cloned.1.call-update) | async-done | bytes 3145744 | tf_op jit(solution)/shard_map/all_gather | solution.py:78
  92.2 14.3 %bitcast_reduce_fusion.1 = (f32[2048,2]{0,1:T(2,128)S(1)}, f32[2048,2]{0,1:T(2,128)S(1)}, f32[2048,2048]{0,1:T(8,128)}) fusion(bf16[2048,768]{1,0:T(8,128)(2,1)} %all-gather.3.cloned.1.call-done, bf16[1024,768]{1,0:T(8,128)(2,1)} %get-tuple-element.10, bf16[1024,768]{1,0:T(8,128)(2,1)S(1)} %get-tuple-element.9), kind=kOutput, calls=%fused_computation.15 | convolution fusion | flops 6465511424 | bytes 23101440 | tf_op jit(solution)/shard_map/dot_general | solution.py:84
  108.6 15.1 %all_to_all.42 = f32[16,1,8192]{2,1,0:T(1,128)S(1)} all-to-all(f32[16,1,8192]{2,1,0:T(1,128)S(1)} %broadcast_in_dim.18), channel_id=1, replica_groups=mesh['row'=8,'col_0'=4,'col_1'=4] {'col_0','col_1'}, dimensions={0} | all-to-all | bytes 1048576 | tf_op jit(solution)/shard_map/all_to_all | solution.py:27
  125.4 8.5 %fusion.5 = (f32[2048]{0:T(1024)S(1)}, f32[2048]{0:T(1024)S(1)}) fusion(f32[2048,2]{0,1:T(2,128)S(1)} %copy.20, f32[2048,2048]{0,1:T(8,128)} %get-tuple-element.17), kind=kLoop, calls=%fused_computation.9 | loop fusion | flops 20967424 | bytes 16809984 | tf_op jit(solution)/shard_map/reduce_sum | solution.py:98
  134.0 10.2 %all_to_all.43 = f32[8,1,4096]{2,1,0:T(1,128)S(1)} all-to-all(f32[8,1,4096]{2,1,0:T(1,128)S(1)} %broadcast_in_dim.19), channel_id=1, replica_groups=mesh['row'=8,'col_0'=4,'col_1'=4] {'row'}, dimensions={0} | all-to-all | bytes 262144 | tf_op jit(solution)/shard_map/all_to_all | solution.py:27
  144.3 7.4 %fusion.6 = f32[2048,2]{0,1:T(2,128)S(1)} fusion(f32[2,1024]{1,0:T(2,128)S(1)} %div.98, f32[2048,2048]{0,1:T(8,128)} %get-tuple-element.17), kind=kLoop, calls=%fused_computation.16 | loop fusion | flops 12578816 | bytes 16801792 | tf_op jit(solution)/shard_map/reduce_sum | solution.py:104
  151.8 11.6 %all_to_all.44 = f32[16,2048,2]{1,2,0:T(2,128)S(1)} all-to-all(f32[16,2048,2]{1,2,0:T(2,128)S(1)} %broadcast_in_dim.20), channel_id=1, replica_groups=mesh['row'=8,'col_0'=4,'col_1'=4] {'col_0','col_1'}, dimensions={0} | all-to-all | bytes 524288 | tf_op jit(solution)/shard_map/all_to_all | solution.py:27
  163.5 8.6 %fusion.4 = f32[2048]{0:T(1024)S(1)} fusion(f32[2048,2]{0,1:T(2,128)S(1)} %broadcast_divide_fusion.1, f32[2048,2048]{0,1:T(8,128)} %get-tuple-element.17), kind=kLoop, calls=%fused_computation.7 | loop fusion | flops 12580864 | bytes 16801792 | tf_op jit(solution)/shard_map/reduce_sum | solution.py:106
  172.2 8.0 %all_to_all.45 = f32[8,2,1024]{2,1,0:T(2,128)S(1)} all-to-all(f32[8,2,1024]{2,1,0:T(2,128)S(1)} %broadcast_in_dim.22), channel_id=1, replica_groups=mesh['row'=8,'col_0'=4,'col_1'=4] {'row'}, dimensions={0} | all-to-all | bytes 131072 | tf_op jit(solution)/shard_map/all_to_all | solution.py:27
  180.2 7.4 %fusion.7 = f32[2048,2]{0,1:T(2,128)S(1)} fusion(f32[2,1024]{1,0:T(2,128)S(1)} %broadcast_divide_fusion.3, f32[2048,2048]{0,1:T(8,128)} %get-tuple-element.17), kind=kLoop, calls=%fused_computation.17 | loop fusion | flops 12578816 | bytes 16801792 | tf_op jit(solution)/shard_map/reduce_sum | solution.py:104
  187.7 11.6 %all_to_all.46 = f32[16,2048,2]{1,2,0:T(2,128)S(1)} all-to-all(f32[16,2048,2]{1,2,0:T(2,128)S(1)} %broadcast_in_dim.23), channel_id=1, replica_groups=mesh['row'=8,'col_0'=4,'col_1'=4] {'col_0','col_1'}, dimensions={0} | all-to-all | bytes 524288 | tf_op jit(solution)/shard_map/all_to_all | solution.py:27
  199.4 8.6 %fusion.10 = f32[2048]{0:T(1024)S(1)} fusion(f32[2048,2]{0,1:T(2,128)S(1)} %broadcast_divide_fusion, f32[2048,2048]{0,1:T(8,128)} %get-tuple-element.17), kind=kLoop, calls=%fused_computation.22 | loop fusion | flops 12580864 | bytes 16801792 | tf_op jit(solution)/shard_map/reduce_sum | solution.py:106
  208.0 8.0 %all_to_all.47 = f32[8,2,1024]{2,1,0:T(2,128)S(1)} all-to-all(f32[8,2,1024]{2,1,0:T(2,128)S(1)} %broadcast_in_dim.25), channel_id=1, replica_groups=mesh['row'=8,'col_0'=4,'col_1'=4] {'row'}, dimensions={0} | all-to-all | bytes 131072 | tf_op jit(solution)/shard_map/all_to_all | solution.py:27
  216.0 7.6 %fusion.9 = f32[2048,2]{0,1:T(2,128)S(1)} fusion(f32[2,1024]{1,0:T(2,128)S(1)} %broadcast_divide_fusion.2, f32[2048,2]{0,1:T(2,128)S(1)} %broadcast_divide_fusion, f32[2048,2048]{0,1:T(8,128)} %get-tuple-element.17), kind=kLoop, calls=%fused_computation.19 | loop fusion | flops 16773120 | bytes 16818176 | tf_op jit(solution)/shard_map/reduce_sum | solution.py:109
  224.5 3.5 %all-to-all-start.6 = ((f32[16,2048,2]{1,2,0:T(2,128)}), f32[16,2048,2]{1,2,0:T(2,128)S(1)}, u32[]{:S(2)}, u32[]{:S(2)}) async-start(f32[16,2048,2]{1,2,0:T(2,128)} %broadcast_in_dim.26), calls=%async_computation.6 | async-start | bytes 524288 | tf_op jit(solution)/shard_map/all_to_all | solution.py:27
  229.6 7.2 %all-to-all-done.6 = f32[16,2048,2]{1,2,0:T(2,128)S(1)} async-done(((f32[16,2048,2]{1,2,0:T(2,128)}), f32[16,2048,2]{1,2,0:T(2,128)S(1)}, u32[]{:S(2)}, u32[]{:S(2)}) %all-to-all-start.6) | async-done | bytes 262176 | tf_op jit(solution)/shard_map/all_to_all | solution.py:27
  236.9 12.1 %fusion.3 = bf16[2048,2048]{0,1:T(8,128)(2,1)S(1)} fusion(f32[2048,2048]{0,1:T(8,128)} %get-tuple-element.17, f32[2048]{0:T(1024)S(1)} %get-tuple-element.16, f32[2048]{0:T(1024)S(1)} %bitcast.56, f32[2048,2]{0,1:T(2,128)S(1)} %reduce_sum.225, f32[2048,2]{0,1:T(2,128)S(1)} %broadcast_divide_fusion, f32[2048,2]{0,1:T(2,128)S(1)} %copy.19), kind=kLoop, calls=%fused_computation.4 | loop fusion | flops 46137344 | bytes 25231360 | tf_op jit(solution)/shard_map/convert_element_type | solution.py:116
  252.2 8.5 %multiply_convert_fusion = bf16[2048,768]{1,0:T(8,128)(2,1)} fusion(bf16[2048,2048]{0,1:T(8,128)(2,1)S(1)} %fusion.3, bf16[1024,768]{1,0:T(8,128)(2,1)S(1)} %copy-done.4, bf16[1024,768]{1,0:T(8,128)(2,1)S(1)} %get-tuple-element.9), kind=kOutput, calls=%fused_computation.27 | convolution fusion | flops 6451888128 | bytes 14680064 | tf_op jit(solution)/shard_map/dot_general | solution.py:119
  260.8 6.3 %fusion.13 = f32[1024,768]{1,0:T(8,128)S(1)} fusion(bf16[2048,768]{1,0:T(8,128)(2,1)} %all-gather.3.cloned.1.call-done, bf16[2048,2048]{0,1:T(8,128)(2,1)} %copy-done), kind=kOutput, calls=%fused_computation.28 | convolution fusion | flops 3221225472 | bytes 10485760 | tf_op jit(solution)/shard_map/dot_general | solution.py:129
  267.9 3.4 %fusion.15 = f32[1024,768]{1,0:T(8,128)S(1)} fusion(bf16[2048,768]{1,0:T(8,128)(2,1)S(1)} %copy-done.5, bf16[2048,2048]{0,1:T(8,128)(2,1)S(1)} %copy-done.1), kind=kOutput, calls=%fused_computation.30 | convolution fusion | flops 3221225472 | bytes 10485760 | tf_op jit(solution)/shard_map/dot_general | solution.py:126
  273.6 3.6 %all-to-all-start.7 = ((bf16[8,128,1536]{2,1,0:T(8,128)(2,1)}), bf16[8,128,1536]{2,1,0:T(8,128)(2,1)S(1)}, u32[]{:S(2)}, u32[]{:S(2)}) async-start(bf16[8,128,1536]{2,1,0:T(8,128)(2,1)} %fusion.12), calls=%async_computation.9 | async-start | bytes 6291456 | tf_op jit(solution)/shard_map/all_to_all | solution.py:60
  277.4 17.7 %reduce-scatter.3.cloned.1.call-done = bf16[512,768]{1,0:T(8,128)(2,1)} async-done(((bf16[2048,768]{1,0:T(8,128)(2,1)}), bf16[512,768]{1,0:T(8,128)(2,1)}) %reduce-scatter.3.cloned.1.call-update) | async-done | bytes 786448 | tf_op jit(solution)/shard_map/reduce_scatter | solution.py:48
  295.1 20.6 %all-to-all-done.7 = bf16[8,128,1536]{2,1,0:T(8,128)(2,1)S(1)} async-done(((bf16[8,128,1536]{2,1,0:T(8,128)(2,1)}), bf16[8,128,1536]{2,1,0:T(8,128)(2,1)S(1)}, u32[]{:S(2)}, u32[]{:S(2)}) %all-to-all-start.7) | async-done | bytes 3145760 | tf_op jit(solution)/shard_map/all_to_all | solution.py:60
  (72 shorter events, 30.5 us)
Async XLA Ops:
  7.2 34.5 %all-gather.5.cloned.1.call-start = ((), (), s32[]{:S(2)}) async-start(), calls=%async_computation.11 | async-start | bytes 3538944 | tf_op jit(solution)/shard_map/all_gather | solution.py:18
  11.3 80.9 %all-gather.3.cloned.1.call-start = ((), (), s32[]{:S(2)}) async-start(), calls=%async_computation.10 | async-start | bytes 3342336 | tf_op jit(solution)/shard_map/all_gather | solution.py:78
  224.5 12.4 %all-to-all-start.6 = ((f32[16,2048,2]{1,2,0:T(2,128)}), f32[16,2048,2]{1,2,0:T(2,128)S(1)}, u32[]{:S(2)}, u32[]{:S(2)}) async-start(f32[16,2048,2]{1,2,0:T(2,128)} %broadcast_in_dim.26), calls=%async_computation.6 | async-start | bytes 524288 | tf_op jit(solution)/shard_map/all_to_all | solution.py:27
  228.0 67.1 %reduce-scatter.3.cloned.1.call-start = ((), (), s32[]{:S(2)}) async-start(), calls=%async_computation.12 | async-start | bytes 3932160 | tf_op jit(solution)/shard_map/reduce_scatter | solution.py:48
  236.9 15.3 %copy-start.4 = (bf16[1024,768]{1,0:T(8,128)(2,1)S(1)}, bf16[1024,768]{1,0:T(8,128)(2,1)}, u32[]{:S(2)}) copy-start(bf16[1024,768]{1,0:T(8,128)(2,1)} %get-tuple-element.10) | copy-start | bytes 4718596
  249.0 3.2 copy-start
  260.8 6.3 %copy-start.1 = (bf16[2048,2048]{0,1:T(8,128)(2,1)S(1)}, bf16[2048,2048]{0,1:T(8,128)(2,1)}, u32[]{:S(2)}) copy-start(bf16[2048,2048]{0,1:T(8,128)(2,1)} %copy-done) | copy-start | bytes 25165828
  260.8 7.0 %copy-start.5 = (bf16[2048,768]{1,0:T(8,128)(2,1)S(1)}, bf16[2048,768]{1,0:T(8,128)(2,1)}, u32[]{:S(2)}) copy-start(bf16[2048,768]{1,0:T(8,128)(2,1)} %all-gather.3.cloned.1.call-done) | copy-start | bytes 9437188
  271.3 44.8 %copy-start.2 = (bf16[128,768]{1,0:T(8,128)(2,1)S(1)}, bf16[128,768]{1,0:T(8,128)(2,1)}, u32[]{:S(2)}) copy-start(bf16[128,768]{1,0:T(8,128)(2,1)} %param.5) | copy-start | bytes 589828
  271.3 44.8 %copy-start.3 = (bf16[128,768]{1,0:T(8,128)(2,1)S(1)}, bf16[128,768]{1,0:T(8,128)(2,1)}, u32[]{:S(2)}) copy-start(bf16[128,768]{1,0:T(8,128)(2,1)} %param.4) | copy-start | bytes 589828
  273.6 42.0 %all-to-all-start.7 = ((bf16[8,128,1536]{2,1,0:T(8,128)(2,1)}), bf16[8,128,1536]{2,1,0:T(8,128)(2,1)S(1)}, u32[]{:S(2)}, u32[]{:S(2)}) async-start(bf16[8,128,1536]{2,1,0:T(8,128)(2,1)} %fusion.12), calls=%async_computation.9 | async-start | bytes 6291456 | tf_op jit(solution)/shard_map/all_to_all | solution.py:60
  277.3 42.1 %reduce-scatter.5.cloned.1.call-start = ((), (), s32[]{:S(2)}) async-start(), calls=%async_computation.13 | async-start | bytes 983040 | tf_op jit(solution)/shard_map/reduce_scatter | solution.py:48
Sparse Core Ops, SparseCore 0:
  11.4 30.1 all-gather.4
  44.3 47.8 all-gather.2
  260.9 34.0 reduce-scatter.2
  297.3 22.0 reduce-scatter.4
where the time goes:
time: 330 us; the launch traced here: 329 us
  waiting for transfers between devices  122 us (37%)
  other arithmetic  75.1 us (23%)
  blocking collectives  64.5 us (20%)
  matrix products  32.5 us (10%)
  between operations  14.1 us (4%)
  local copies, waits for them, and re-layouts  13.1 us (4%)
  starting transfers between devices  7.57 us (2%)
    all_to_all x6, blocking collectives, from_everyone(): lax.all_to_all(jnp.broadcast_to(value[None], (size, *value.shape)), axis,...  64.5 us
    all_gather x1, waiting for transfers between devices, shards(): lax.all_gather(img_unit.astype(jnp.bfloat16), COL, axis=0, tiled=True)  47.4 us
    all_gather x1, waiting for transfers between devices, in_one_piece(): filled, at, outs = (lax.all_gather(both, axis, axis=dim, tiled=True), 0, [])  27.5 us
    reduce_sum x3, other arithmetic, shards(): jnp.sum(loss_routine * rows_scale[:, :, None], axis=0)  25.7 us
    all_to_all x1, waiting for transfers between devices, summed_on_arrival(): lax.all_to_all(blocks, axis, split_axis=0, concat_axis=0, tiled=True)  20.6 us
    reduce_scatter x2, waiting for transfers between devices, summed_rows(): subtotal = lax.psum_scatter(subtotal, axis, scatter_dimension=0, tiled=True)  19.7 us
    reduce_sum x2, other arithmetic, shards(): jnp.sum(loss_routine * cols_scale[None], axis=2)  14.7 us
    dot_general x1, matrix products, shards(): lax.dot_general(img_rows, paired_cols, contract, preferred_element_type=j...  14.3 us
  transfers between devices with their start and end apart: 6, of which 6 were waited for; matrix products, arithmetic and copies ran while one was open for 6% of the time, Pallas kernels for 0%

commit v1 on v0

--- a/solution.py
+++ b/solution.py
@@ -1,3 +1,4 @@
+import functools
 import jax
 import jax.numpy as jnp
 from jax import lax
@@ -11,6 +12,21 @@
 logit_softness = 0.07
 target_softness = 0.05
 epsilon = 1e-06
+
+
+def raise_the_slices(field, row_axis):
+    return jnp.concatenate(
+        jax.lax.all_to_all(
+            jnp.stack(tuple((field for _ in range(jax.lax.psum(1, row_axis)))), axis=0),
+            axis_name=row_axis,
+            split_axis=0,
+            concat_axis=0,
+        ),
+        0,
+    )
+
+
+move_unit = functools.partial(raise_the_slices, row_axis=COL)
 
 
 def in_one_piece(arrays, axis, dim, along):
@@ -75,7 +91,7 @@
     img_unit, img_inverse = normalize(images)
     txt_unit, txt_inverse = normalize(texts)
     aud_unit, aud_inverse = normalize(audio)
-    img_rows = lax.all_gather(img_unit.astype(jnp.bfloat16), COL, axis=0, tiled=True)
+    img_rows = move_unit(img_unit.astype(jnp.bfloat16))
     text_columns, audio_columns = in_one_piece(
         (txt_unit.astype(jnp.bfloat16), aud_unit.astype(jnp.bfloat16)), "row", 0, 1
     )

time: 330 us -> 309 us (0.936)
  waiting for transfers between devices: 122 us -> 90.7 us
  starting transfers between devices: 7.57 us -> 15.5 us
  local copies, waits for them, and re-layouts: 13.1 us -> 19.3 us
    all_gather x1 -> x0, waiting for transfers between devices: 47.4 us -> none  [shards(): lax.all_gather(img_unit.astype(jnp.bfloat16), COL, axis=0, tiled=True)]
    all_to_all x0 -> x1, waiting for transfers between devices: none -> 25.6 us  [raise_the_slices(): jax.lax.all_to_all(jnp.stack(tuple((field for _ in range(jax.lax.psum(1,...]
    all_gather x1, waiting for transfers between devices: 27.5 us -> 18.2 us  [in_one_piece(): filled, at, outs = (lax.all_gather(both, axis, axis=dim, tiled=True), 0, [])]
    all_to_all x0 -> x1, starting transfers between devices: none -> 7.99 us  [raise_the_slices(): jax.lax.all_to_all(jnp.stack(tuple((field for _ in range(jax.lax.psum(1,...]
    slice x0 -> x1, local copies, waits for them, and re-layouts: none -> 4.4 us  [shards(): lax.slice_in_dim(score_matrix, 0, owned * lax.axis_size('row'), axis=1)]
  transfers between devices with their start and end apart: 6 -> 6, of which waited for: 6 -> 6; matrix products, arithmetic and copies ran while one was open for 6% -> 8% of each run, Pallas kernels for 0% -> 0%
where the time goes in v1:
time: 309 us; the launch traced here: 308 us
  waiting for transfers between devices  90.7 us (29%)
  other arithmetic  74.5 us (24%)
  blocking collectives  64.2 us (21%)
  matrix products  29.9 us (10%)
  local copies, waits for them, and re-layouts  19.3 us (6%)
  starting transfers between devices  15.5 us (5%)
  between operations  14.1 us (5%)
    all_to_all x6, blocking collectives, from_everyone(): lax.all_to_all(jnp.broadcast_to(value[None], (size, *value.shape)), axis,...  64.2 us
    reduce_sum x3, other arithmetic, shards(): jnp.sum(loss_routine * rows_scale[:, :, None], axis=0)  25.7 us
    all_to_all x1, waiting for transfers between devices, raise_the_slices(): jax.lax.all_to_all(jnp.stack(tuple((field for _ in range(jax.lax.psum(1,...  25.6 us
    all_to_all x1, waiting for transfers between devices, summed_on_arrival(): lax.all_to_all(blocks, axis, split_axis=0, concat_axis=0, tiled=True)  21.4 us
    all_gather x1, waiting for transfers between devices, in_one_piece(): filled, at, outs = (lax.all_gather(both, axis, axis=dim, tiled=True), 0, [])  18.2 us
    reduce_scatter x2, waiting for transfers between devices, summed_rows(): subtotal = lax.psum_scatter(subtotal, axis, scatter_dimension=0, tiled=True)  18.2 us
    reduce_sum x2, other arithmetic, shards(): jnp.sum(loss_routine * cols_scale[None], axis=2)  14.7 us
    dot_general x1, matrix products, shards(): lax.dot_general(img_rows, paired_cols, contract, preferred_element_type=j...  14.5 us
  transfers between devices with their start and end apart: 6, of which 6 were waited for; matrix products, arithmetic and copies ran while one was open for 8% of the time, Pallas kernels for 0%

profile of v1, /device:TPU:0, one launch (start us, length us, event | category | flops | bytes accessed | tf_op | source)
XLA Modules:
  0.0 308.2 jit_solution(10593426790250327959)
XLA Ops:
  15.4 8.0 %all-to-all-start = ((bf16[16,128,768]{2,1,0:T(8,128)(2,1)}), bf16[16,128,768]{2,1,0:T(8,128)(2,1)S(1)}, u32[]{:S(2)}, u32[]{:S(2)}) async-start(bf16[16,128,768]{2,1,0:T(8,128)(2,1)} %stack.2), calls=%async_computation | async-start | bytes 6291456 | tf_op jit(solution)/shard_map/all_to_all | solution.py:19
  23.4 18.2 %all-gather.2.cloned.1.call-done = bf16[1024,1536]{1,0:T(8,128)(2,1)} async-done(((bf16[128,1536]{1,0:T(8,128)(2,1)}), bf16[1024,1536]{1,0:T(8,128)(2,1)}) %all-gather.2.cloned.1.call-update) | async-done | bytes 3145744 | tf_op jit(solution)/shard_map/all_gather | solution.py:34
  41.6 3.8 %fusion.36 = (bf16[1024,768]{1,0:T(8,128)(2,1)}, bf16[1024,768]{1,0:T(8,128)(2,1)}) fusion(bf16[1024,1536]{1,0:T(8,128)(2,1)} %all-gather.2.cloned.1.call-done), kind=kLoop, calls=%fused_computation.73 | loop fusion | bytes 6291456 | tf_op jit(solution)/shard_map/slice | solution.py:36
  45.4 25.6 %all-to-all-done = bf16[16,128,768]{2,1,0:T(8,128)(2,1)S(1)} async-done(((bf16[16,128,768]{2,1,0:T(8,128)(2,1)}), bf16[16,128,768]{2,1,0:T(8,128)(2,1)S(1)}, u32[]{:S(2)}, u32[]{:S(2)}) %all-to-all-start) | async-done | bytes 3145760 | tf_op jit(solution)/shard_map/all_to_all | solution.py:19
  71.0 14.5 %bitcast_reduce_fusion.1 = (f32[2048,2]{0,1:T(2,128)S(1)}, f32[2048,2]{0,1:T(2,128)S(1)}, f32[2048,2048]{0,1:T(8,128)}) fusion(bf16[2048,768]{1,0:T(8,128)(2,1)S(1)} %bitcast.65, bf16[1024,768]{1,0:T(8,128)(2,1)} %get-tuple-element.12, bf16[1024,768]{1,0:T(8,128)(2,1)} %get-tuple-element.11), kind=kOutput, calls=%fused_computation.15 | convolution fusion | flops 6465511424 | bytes 23101440 | tf_op jit(solution)/shard_map/dot_general | solution.py:100
  87.7 14.6 %all_to_all.47 = f32[16,1,8192]{2,1,0:T(1,128)S(1)} all-to-all(f32[16,1,8192]{2,1,0:T(1,128)S(1)} %broadcast_in_dim.18), channel_id=1, replica_groups=mesh['row'=8,'col_0'=4,'col_1'=4] {'col_0','col_1'}, dimensions={0} | all-to-all | bytes 1048576 | tf_op jit(solution)/shard_map/all_to_all | solution.py:43
  104.0 8.5 %fusion.5 = (f32[2048]{0:T(1024)S(1)}, f32[2048]{0:T(1024)S(1)}) fusion(f32[2048,2]{0,1:T(2,128)S(1)} %copy.20, f32[2048,2048]{0,1:T(8,128)} %get-tuple-element.19), kind=kLoop, calls=%fused_computation.9 | loop fusion | flops 20967424 | bytes 16809984 | tf_op jit(solution)/shard_map/reduce_sum | solution.py:114
  112.6 10.4 %all_to_all.48 = f32[8,1,4096]{2,1,0:T(1,128)S(1)} all-to-all(f32[8,1,4096]{2,1,0:T(1,128)S(1)} %broadcast_in_dim.19), channel_id=1, replica_groups=mesh['row'=8,'col_0'=4,'col_1'=4] {'row'}, dimensions={0} | all-to-all | bytes 262144 | tf_op jit(solution)/shard_map/all_to_all | solution.py:43
  123.1 7.4 %fusion.6 = f32[2048,2]{0,1:T(2,128)S(1)} fusion(f32[2,1024]{1,0:T(2,128)S(1)} %div.98, f32[2048,2048]{0,1:T(8,128)} %get-tuple-element.19), kind=kLoop, calls=%fused_computation.16 | loop fusion | flops 12578816 | bytes 16801792 | tf_op jit(solution)/shard_map/reduce_sum | solution.py:120
  130.6 11.6 %all_to_all.49 = f32[16,2048,2]{1,2,0:T(2,128)S(1)} all-to-all(f32[16,2048,2]{1,2,0:T(2,128)S(1)} %broadcast_in_dim.20), channel_id=1, replica_groups=mesh['row'=8,'col_0'=4,'col_1'=4] {'col_0','col_1'}, dimensions={0} | all-to-all | bytes 524288 | tf_op jit(solution)/shard_map/all_to_all | solution.py:43
  142.3 8.6 %fusion.4 = f32[2048]{0:T(1024)S(1)} fusion(f32[2048,2]{0,1:T(2,128)S(1)} %broadcast_divide_fusion.1, f32[2048,2048]{0,1:T(8,128)} %get-tuple-element.19), kind=kLoop, calls=%fused_computation.7 | loop fusion | flops 12580864 | bytes 16801792 | tf_op jit(solution)/shard_map/reduce_sum | solution.py:122
  151.0 8.0 %all_to_all.50 = f32[8,2,1024]{2,1,0:T(2,128)S(1)} all-to-all(f32[8,2,1024]{2,1,0:T(2,128)S(1)} %broadcast_in_dim.22), channel_id=1, replica_groups=mesh['row'=8,'col_0'=4,'col_1'=4] {'row'}, dimensions={0} | all-to-all | bytes 131072 | tf_op jit(solution)/shard_map/all_to_all | solution.py:43
  159.0 7.4 %fusion.7 = f32[2048,2]{0,1:T(2,128)S(1)} fusion(f32[2,1024]{1,0:T(2,128)S(1)} %broadcast_divide_fusion.3, f32[2048,2048]{0,1:T(8,128)} %get-tuple-element.19), kind=kLoop, calls=%fused_computation.17 | loop fusion | flops 12578816 | bytes 16801792 | tf_op jit(solution)/shard_map/reduce_sum | solution.py:120
  166.5 11.6 %all_to_all.51 = f32[16,2048,2]{1,2,0:T(2,128)S(1)} all-to-all(f32[16,2048,2]{1,2,0:T(2,128)S(1)} %broadcast_in_dim.23), channel_id=1, replica_groups=mesh['row'=8,'col_0'=4,'col_1'=4] {'col_0','col_1'}, dimensions={0} | all-to-all | bytes 524288 | tf_op jit(solution)/shard_map/all_to_all | solution.py:43
  178.2 8.6 %fusion.10 = f32[2048]{0:T(1024)S(1)} fusion(f32[2048,2]{0,1:T(2,128)S(1)} %broadcast_divide_fusion, f32[2048,2048]{0,1:T(8,128)} %get-tuple-element.19), kind=kLoop, calls=%fused_computation.22 | loop fusion | flops 12580864 | bytes 16801792 | tf_op jit(solution)/shard_map/reduce_sum | solution.py:122
  186.8 8.0 %all_to_all.52 = f32[8,2,1024]{2,1,0:T(2,128)S(1)} all-to-all(f32[8,2,1024]{2,1,0:T(2,128)S(1)} %broadcast_in_dim.25), channel_id=1, replica_groups=mesh['row'=8,'col_0'=4,'col_1'=4] {'row'}, dimensions={0} | all-to-all | bytes 131072 | tf_op jit(solution)/shard_map/all_to_all | solution.py:43
  194.8 7.6 %fusion.9 = f32[2048,2]{0,1:T(2,128)S(1)} fusion(f32[2,1024]{1,0:T(2,128)S(1)} %broadcast_divide_fusion.2, f32[2048,2]{0,1:T(2,128)S(1)} %broadcast_divide_fusion, f32[2048,2048]{0,1:T(8,128)} %get-tuple-element.19), kind=kLoop, calls=%fused_computation.19 | loop fusion | flops 16773120 | bytes 16818176 | tf_op jit(solution)/shard_map/reduce_sum | solution.py:125
  208.4 7.2 %all-to-all-done.7 = f32[16,2048,2]{1,2,0:T(2,128)S(1)} async-done(((f32[16,2048,2]{1,2,0:T(2,128)}), f32[16,2048,2]{1,2,0:T(2,128)S(1)}, u32[]{:S(2)}, u32[]{:S(2)}) %all-to-all-start.7) | async-done | bytes 262176 | tf_op jit(solution)/shard_map/all_to_all | solution.py:43
  215.7 12.1 %fusion.3 = bf16[2048,2048]{0,1:T(8,128)(2,1)S(1)} fusion(f32[2048,2048]{0,1:T(8,128)} %get-tuple-element.19, f32[2048]{0:T(1024)S(1)} %get-tuple-element.18, f32[2048]{0:T(1024)S(1)} %bitcast.68, f32[2048,2]{0,1:T(2,128)S(1)} %reduce_sum.225, f32[2048,2]{0,1:T(2,128)S(1)} %broadcast_divide_fusion, f32[2048,2]{0,1:T(2,128)S(1)} %copy.19), kind=kLoop, calls=%fused_computation.4 | loop fusion | flops 46137344 | bytes 25231360 | tf_op jit(solution)/shard_map/convert_element_type | solution.py:132
  231.1 8.6 %multiply_convert_fusion = bf16[2048,768]{1,0:T(8,128)(2,1)} fusion(bf16[2048,2048]{0,1:T(8,128)(2,1)S(1)} %fusion.3, bf16[1024,768]{1,0:T(8,128)(2,1)S(1)} %copy-done.6, bf16[1024,768]{1,0:T(8,128)(2,1)S(1)} %copy-done.5), kind=kOutput, calls=%fused_computation.27 | convolution fusion | flops 6451888128 | bytes 14680064 | tf_op jit(solution)/shard_map/dot_general | solution.py:135
  239.7 4.4 %fusion.35 = (bf16[2048,1024]{0,1:T(8,128)(2,1)S(1)}, bf16[2048,1024]{0,1:T(8,128)(2,1)S(1)}) fusion(bf16[2048,2048]{0,1:T(8,128)(2,1)} %copy-done), kind=kLoop, calls=%fused_computation.72 | loop fusion | bytes 16777216 | tf_op jit(solution)/shard_map/slice | solution.py:137
  253.3 3.7 %all-to-all-start.8 = ((bf16[8,128,1536]{2,1,0:T(8,128)(2,1)}), bf16[8,128,1536]{2,1,0:T(8,128)(2,1)S(1)}, u32[]{:S(2)}, u32[]{:S(2)}) async-start(bf16[8,128,1536]{2,1,0:T(8,128)(2,1)} %fusion.12), calls=%async_computation.10 | async-start | bytes 6291456 | tf_op jit(solution)/shard_map/all_to_all | solution.py:76
  257.1 16.8 %reduce-scatter.3.cloned.1.call-done = bf16[512,768]{1,0:T(8,128)(2,1)} async-done(((bf16[2048,768]{1,0:T(8,128)(2,1)}), bf16[512,768]{1,0:T(8,128)(2,1)}) %reduce-scatter.3.cloned.1.call-update) | async-done | bytes 786448 | tf_op jit(solution)/shard_map/reduce_scatter | solution.py:64
  273.9 21.4 %all-to-all-done.8 = bf16[8,128,1536]{2,1,0:T(8,128)(2,1)S(1)} async-done(((bf16[8,128,1536]{2,1,0:T(8,128)(2,1)}), bf16[8,128,1536]{2,1,0:T(8,128)(2,1)S(1)}, u32[]{:S(2)}, u32[]{:S(2)}) %all-to-all-start.8) | async-done | bytes 3145760 | tf_op jit(solution)/shard_map/all_to_all | solution.py:76
  (75 shorter events, 37.6 us)
Async XLA Ops:
  7.2 34.5 %all-gather.2.cloned.1.call-start = ((), (), s32[]{:S(2)}) async-start(), calls=%async_computation.11 | async-start | bytes 3538944 | tf_op jit(solution)/shard_map/all_gather | solution.py:34
  15.4 55.6 %all-to-all-start = ((bf16[16,128,768]{2,1,0:T(8,128)(2,1)}), bf16[16,128,768]{2,1,0:T(8,128)(2,1)S(1)}, u32[]{:S(2)}, u32[]{:S(2)}) async-start(bf16[16,128,768]{2,1,0:T(8,128)(2,1)} %stack.2), calls=%async_computation | async-start | bytes 6291456 | tf_op jit(solution)/shard_map/all_to_all | solution.py:19
  71.0 14.5 %copy-start.1 = (bf16[16,128,768]{2,1,0:T(8,128)(2,1)}, bf16[16,128,768]{2,1,0:T(8,128)(2,1)S(1)}, u32[]{:S(2)}) copy-start(bf16[16,128,768]{2,1,0:T(8,128)(2,1)S(1)} %all-to-all-done) | copy-start | bytes 9437188
  203.2 12.4 %all-to-all-start.7 = ((f32[16,2048,2]{1,2,0:T(2,128)}), f32[16,2048,2]{1,2,0:T(2,128)S(1)}, u32[]{:S(2)}, u32[]{:S(2)}) async-start(f32[16,2048,2]{1,2,0:T(2,128)} %broadcast_in_dim.26), calls=%async_computation.7 | async-start | bytes 524288 | tf_op jit(solution)/shard_map/all_to_all | solution.py:43
  206.8 67.1 %reduce-scatter.3.cloned.1.call-start = ((), (), s32[]{:S(2)}) async-start(), calls=%async_computation.12 | async-start | bytes 3932160 | tf_op jit(solution)/shard_map/reduce_scatter | solution.py:64
  215.7 15.4 %copy-start.5 = (bf16[1024,768]{1,0:T(8,128)(2,1)S(1)}, bf16[1024,768]{1,0:T(8,128)(2,1)}, u32[]{:S(2)}) copy-start(bf16[1024,768]{1,0:T(8,128)(2,1)} %get-tuple-element.11) | copy-start | bytes 4718596
  215.7 15.4 %copy-start.6 = (bf16[1024,768]{1,0:T(8,128)(2,1)S(1)}, bf16[1024,768]{1,0:T(8,128)(2,1)}, u32[]{:S(2)}) copy-start(bf16[1024,768]{1,0:T(8,128)(2,1)} %get-tuple-element.12) | copy-start | bytes 4718596
  227.8 3.2 %copy-start = (bf16[2048,2048]{0,1:T(8,128)(2,1)}, bf16[2048,2048]{0,1:T(8,128)(2,1)S(1)}, u32[]{:S(2)}) copy-start(bf16[2048,2048]{0,1:T(8,128)(2,1)S(1)} %fusion.3) | copy-start | bytes 25165828
  239.7 4.4 %copy-start.2 = (bf16[16,128,768]{2,1,0:T(8,128)(2,1)S(1)}, bf16[16,128,768]{2,1,0:T(8,128)(2,1)}, u32[]{:S(2)}) copy-start(bf16[16,128,768]{2,1,0:T(8,128)(2,1)} %copy-done.1) | copy-start | bytes 9437188
  250.9 44.8 %copy-start.3 = (bf16[128,768]{1,0:T(8,128)(2,1)S(1)}, bf16[128,768]{1,0:T(8,128)(2,1)}, u32[]{:S(2)}) copy-start(bf16[128,768]{1,0:T(8,128)(2,1)} %param.5) | copy-start | bytes 589828
  251.0 44.8 %copy-start.4 = (bf16[128,768]{1,0:T(8,128)(2,1)S(1)}, bf16[128,768]{1,0:T(8,128)(2,1)}, u32[]{:S(2)}) copy-start(bf16[128,768]{1,0:T(8,128)(2,1)} %param.4) | copy-start | bytes 589828
  253.3 42.0 %all-to-all-start.8 = ((bf16[8,128,1536]{2,1,0:T(8,128)(2,1)}), bf16[8,128,1536]{2,1,0:T(8,128)(2,1)S(1)}, u32[]{:S(2)}, u32[]{:S(2)}) async-start(bf16[8,128,1536]{2,1,0:T(8,128)(2,1)} %fusion.12), calls=%async_computation.10 | async-start | bytes 6291456 | tf_op jit(solution)/shard_map/all_to_all | solution.py:76
  257.0 41.5 %reduce-scatter.5.cloned.1.call-start = ((), (), s32[]{:S(2)}) async-start(), calls=%async_computation.13 | async-start | bytes 983040 | tf_op jit(solution)/shard_map/reduce_scatter | solution.py:64
Sparse Core Ops, SparseCore 0:
  11.4 30.1 all-gather.1
  239.8 34.0 reduce-scatter.2
  276.3 22.1 reduce-scatter.4
